TPU v7x, 32 devices: a whole 2x2x4 slice. The times are simulated.
32 devices in a mesh: azi: 8 (over z, core), ax: 2 (over y), rad: 2 (over x).
Axes of the slice: x: 2, y: 2, z: 4, core: 2. Of those that a mesh axis runs over, the one named last changes fastest.
Arguments:
- fields: float32 [2, 512, 32, 1024], P(None, 'azi', 'ax', 'rad'), may hold values from 0 to 1.5
- swirl_speed: float32 [512, 32, 1024], P('azi', 'ax', 'rad'), may hold values from 0.05 to 0.35
- ghost_mask: int32 [512, 32, 1024], P('azi', 'ax', 'rad'), may hold values 0 or 1
- tile_flags: int32 [32, 32], P('azi', 'ax'), may hold values 0 or 1
- outlet_gain: float32 [2, 32], replicated, may hold values from 0.25 to 1
- feed_rate: float32 [8, 8, 8], P('azi'), may hold values from 0.05 to 0.5
- plenum: float32 [8, 8, 8, 1024], P('azi', None, None, 'rad'), may hold values from 0.5 to 1.5
- feed_target: int32 [8, 8, 8], P('azi'), may hold values from -1 to 255, as said below
Outputs:
- new_fields: float32 [2, 512, 32, 1024], P(None, 'azi', 'ax', 'rad')
Inputs may be any that keep to these rules, and one draw needn't show every extreme that they name: `feed_target`: entry i >= 0 names azimuthal cell i // 4 and axial cell i mod 4 of sector d; -1 marks an empty slot, and the used slots of a pair come first. At most 8 slots per pair are used; in every draw one sector receives 8 from every sector.
All inputs are finite; a program needn't handle non-finite values. No bound on the sum of `ghost_mask` or of `tile_flags` on one device may be relied on, other than what follows from the above.
Results may differ from a plain program's by a relative error of at most 0.00005.
Values sent between devices are 32-bit elements; how exact they have to be, the bound alone decides.
No kernel may reach another device: no remote copies, remote signals or barrier semaphores. Data moves between devices by JAX's collectives and lax.ppermute only.
A program may use at most 64 MiB of HBM per device.

v0:
```python
import math
import jax
import jax.numpy as jnp
from jax import lax
from jax.sharding import PartitionSpec as P

K = 32
TILE = 16
HEAD = 4


def with_halo(block, sides, width, periodic):
    for axis, dim in sides:
        count = lax.axis_size(axis)
        forward = [(i, i + 1) for i in range(count - 1)]
        if periodic:
            forward.append((count - 1, 0))
        backward = [(target, source) for source, target in forward]
        low = lax.ppermute(
            lax.slice_in_dim(block, block.shape[dim] - width, None, axis=dim), axis, forward
        )
        high = lax.ppermute(lax.slice_in_dim(block, 0, width, axis=dim), axis, backward)
        block = jnp.concatenate([low, block, high], axis=dim)
    return block


def phase_table(length, first_cell, cell_count, mode_count):
    theta_index = first_cell + jnp.arange(cell_count, dtype=jnp.int32)
    mode_order = jnp.arange(1, mode_count + 1, dtype=jnp.int32)
    phase_int = mode_order[:, None] * theta_index[None, :] % length
    angles = phase_int.astype(jnp.float32) * (2.0 * math.pi / length)
    return jnp.concatenate([jnp.cos(angles), jnp.sin(angles)], axis=0)


def body(fields, swirl_speed, ghost_mask, tile_flags, outlet_gain, feed_rate, plenum, feed_target):
    sectors = lax.axis_size("azi")
    sector = lax.axis_index("azi")
    slab_index = lax.axis_index("ax")
    slab_count = lax.axis_size("ax")
    sector_cells = fields.shape[1]
    depth_cells = fields.shape[2]
    radial_cells = fields.shape[3]
    length = sector_cells * sectors
    phase_rows = phase_table(length, sector * sector_cells, sector_cells, K)
    outlet_plane = fields[:, :, -1, :]
    partial_value = jnp.einsum(
        "mt,ctr->cmr", phase_rows, outlet_plane, precision=lax.Precision.HIGHEST
    )
    gain_both = jnp.concatenate([outlet_gain, outlet_gain], axis=1)
    mode_sums = lax.psum(partial_value, "azi")
    rebuilt = jnp.einsum(
        "mt,cmr->ctr",
        phase_rows,
        mode_sums * gain_both[:, :, None],
        precision=lax.Precision.HIGHEST,
    )
    ghost_plane = outlet_plane - rebuilt * (2.0 / math.sqrt(K * length))
    azimuth_pad = with_halo(fields, (("azi", 1),), 1, True)
    face_pad = with_halo(fields, (("ax", 2), ("rad", 3)), 1, False)
    theta_prev = azimuth_pad[:, :-2]
    theta_next = azimuth_pad[:, 2:]
    axial_prev = face_pad[:, :, :-2, 1:-1]
    axial_inner = face_pad[:, :, 2:, 1:-1]
    radial_prev = face_pad[:, :, 1:-1, :-2]
    radial_next = face_pad[:, :, 1:-1, 2:]
    is_outlet = slab_index == slab_count - 1
    top_layer = jnp.where(is_outlet, ghost_plane, axial_inner[:, :, -1, :])
    axial_next = jnp.concatenate([axial_inner[:, :, :-1, :], top_layer[:, :, None, :]], axis=2)
    laplace_term = (
        theta_prev + theta_next + axial_prev + axial_next + radial_prev + radial_next - 6.0 * fields
    )
    upwind_term = swirl_speed[None] * (fields - theta_prev)
    energy = fields[0]
    fuel_part = fields[1]
    tile_on = jnp.repeat(tile_flags, TILE, axis=0).astype(jnp.float32)
    inert = ghost_mask.astype(jnp.float32)
    reaction = (
        0.5 * tile_on[:, :, None] * (1.0 - inert) * fuel_part * jax.nn.sigmoid(4.0 * (energy - 0.5))
    )
    payload = feed_rate[0][:, :, None] * plenum[0]
    arrived = lax.all_to_all(payload, "azi", split_axis=0, concat_axis=0, tiled=True)
    targets = feed_target[0]
    occupied = targets >= 0
    row_index = jnp.where(
        occupied, targets // HEAD * depth_cells + targets % HEAD, sector_cells * depth_cells
    )
    feed_term = jnp.zeros((sector_cells * depth_cells, radial_cells), jnp.float32)
    feed_term = feed_term.at[row_index.reshape(-1)].add(
        arrived.reshape(-1, radial_cells), mode="drop"
    )
    feed_term = feed_term.reshape(sector_cells, depth_cells, radial_cells) * (
        slab_index == 0
    ).astype(jnp.float32)
    new_energy = energy - upwind_term[0] + 0.1 * laplace_term[0] + 2.0 * reaction
    new_fuel = fuel_part - upwind_term[1] + 0.1 * laplace_term[1] - reaction + feed_term
    return jnp.stack([new_energy, new_fuel], axis=0)


def solution(mesh):
    return jax.shard_map(
        body,
        mesh=mesh,
        in_specs=(
            P(None, "azi", "ax", "rad"),
            P("azi", "ax", "rad"),
            P("azi", "ax", "rad"),
            P("azi", "ax"),
            P(),
            P("azi", None, None),
            P("azi", None, None, "rad"),
            P("azi", None, None),
        ),
        out_specs=P(None, "azi", "ax", "rad"),
        check_vma=False,
    )
```

profile of v0, /device:TPU:0, one launch (start us, length us, event | category | flops | bytes accessed | tf_op | source)
XLA Modules:
  0.0 102.9 jit_solution(10300405495476792824)
XLA Ops:
  6.5 2.8 %fusion.38 = (f32[2,64,1,512]{3,2,1,0:T(1,128)S(1)}, f32[2,64,1,512]{3,2,1,0:T(1,128)S(1)}) fusion(f32[2,64,16,512]{3,2,1,0:T(8,128)} %param.8), kind=kLoop, calls=%fused_computation.80 | loop fusion | bytes 1048576 | tf_op jit(solution)/shard_map/slice | solution.py:20
  9.3 0.2 fusion.31
  9.5 1.1 %convolution_bitcast_fusion = f32[2,64,512]{2,1,0:T(8,128)} fusion(f32[32,64]{1,0:T(8,128)S(1)} %get-tuple-element.14, f32[32,64]{1,0:T(8,128)S(1)} %get-tuple-element.13, f32[2,64,1,512]{3,2,1,0:T(1,128)S(1)} %get-tuple-element.11), kind=kOutput, calls=%fused_computation.41 | convolution fusion | flops 50335744 | bytes 540672 | tf_op jit(solution)/shard_map/mt,ctr->cmr/dot_general | solution.py:46
  10.6 1.3 %collective-permute-start.3 = (f32[2,64,1,512]{3,1,0,2:T(8,128)S(1)}, f32[2,64,1,512]{3,1,0,2:T(8,128)S(1)}, u32[]{:S(2)}, u32[]{:S(2)}) collective-permute-start(f32[2,64,1,512]{3,1,0,2:T(8,128)S(1)} %copy.56), channel_id=1, source_target_pairs={{2,0},{3,1},{6,4},{7,5},{10,8},{11,9},{14,12},{15,13},{18,16},{19,... | collective-permute-start | bytes 786440 | tf_op jit(solution)/shard_map/ppermute | solution.py:22
  11.9 0.7 copy.55
  12.7 4.9 %collective-permute-start.2 = (f32[2,64,1,512]{3,1,0,2:T(8,128)}, f32[2,64,1,512]{3,1,0,2:T(8,128)S(1)}, u32[]{:S(2)}, u32[]{:S(2)}) collective-permute-start(f32[2,64,1,512]{3,1,0,2:T(8,128)} %copy.55), channel_id=1, source_target_pairs={{0,2},{1,3},{4,6},{5,7},{8,10},{9,11},{12,14},{13,15},{16,18},{17,... | collective-permute-start | bytes 786440 | tf_op jit(solution)/shard_map/ppermute | solution.py:19
  17.6 1.5 %fusion.37 = (f32[2,1,16,512]{3,2,1,0:T(8,128)S(1)}, f32[2,1,16,512]{3,2,1,0:T(8,128)}) fusion(f32[2,64,16,512]{3,2,1,0:T(8,128)} %param.8), kind=kLoop, calls=%fused_computation.79 | loop fusion | bytes 262144 | tf_op jit(solution)/shard_map/slice | solution.py:20
  19.1 3.6 %collective-permute-start.1 = (f32[2,1,16,512]{3,2,1,0:T(8,128)}, f32[2,1,16,512]{3,2,1,0:T(8,128)}, u32[]{:S(2)}, u32[]{:S(2)}) collective-permute-start(f32[2,1,16,512]{3,2,1,0:T(8,128)} %get-tuple-element.10), channel_id=1, source_target_pairs={{4,0},{8,4},{12,8},{16,12},{20,16},{24,20},{28,24},{0,28},{5,1},{9... | collective-permute-start | bytes 196616 | tf_op jit(solution)/shard_map/ppermute | solution.py:22
  22.7 0.7 bitcast_multiply_fusion.2
  23.5 4.1 %all-to-all-start = ((f32[8,8,512]{2,1,0:T(8,128)}), f32[8,8,512]{2,1,0:T(8,128)S(1)}, u32[]{:S(2)}, u32[]{:S(2)}) async-start(f32[8,8,512]{2,1,0:T(8,128)} %bitcast_multiply_fusion.2), calls=%async_computation | async-start | bytes 262144 | tf_op jit(solution)/shard_map/all_to_all | solution.py:81
  27.6 5.2 %slice.74 = f32[2,64,15,512]{3,2,1,0:T(8,128)} slice(f32[2,64,16,512]{3,2,1,0:T(8,128)} %param.8), slice={[0:2], [0:64], [1:16], [0:512]} | slice | bytes 7864320 | tf_op jit(solution)/shard_map/slice | solution.py:68
  33.1 6.9 %fusion.7 = f32[2,64,16,512]{3,2,1,0:T(8,128)} fusion(f32[2,64,16,512]{3,2,1,0:T(8,128)} %param.8, f32[2,1,16,512]{3,2,1,0:T(8,128)S(1)} %collective-permute-done, f32[64,16,512]{2,1,0:T(8,128)S(1)} %copy-done.7), kind=kLoop, calls=%fused_computation.17 | loop fusion | flops 3145728 | bytes 10551296 | tf_op jit(solution)/shard_map/mul | solution.py:72
  40.0 1.5 %scatter_custom_fusion = f32[1024,512]{1,0:T(8,128)S(1)} fusion(s32[64]{0:T(128)S(1)} %fusion.33, f32[]{:T(128)} %constant.78.clone.1, f32[8,8,512]{2,1,0:T(8,128)S(1)} %all-to-all-done), kind=kCustom, calls=%fused_computation.43 | custom fusion | flops 32768 | bytes 2228228 | tf_op jit(solution)/shard_map/scatter-add | solution.py:88
  41.5 1.6 %broadcast_multiply_fusion = f32[1024,512]{1,0:T(8,128)} fusion(f32[1024,512]{1,0:T(8,128)S(1)} %scatter_custom_fusion, f32[]{:T(128)S(6)} %convert_element_type.21), kind=kLoop, calls=%fused_computation.42 | loop fusion | flops 524288 | bytes 4194308 | tf_op jit(solution)/shard_map/mul | solution.py:91
  43.1 0.3 copy.43
  43.4 0.7 copy-done.8
  44.1 0.3 copy.48
  44.4 0.3 copy-done
  44.7 1.0 pad_maximum_fusion.12
  45.7 0.5 copy.49
  46.1 3.7 %collective-permute-start.4 = (f32[2,64,18,1]{1,0,3,2:T(2,128)S(1)}, f32[2,64,18,1]{1,0,3,2:T(2,128)S(1)}, u32[]{:S(2)}, u32[]{:S(2)}) collective-permute-start(f32[2,64,18,1]{1,0,3,2:T(2,128)S(1)} %copy.49), channel_id=1, source_target_pairs={{0,1},{2,3},{4,5},{6,7},{8,9},{10,11},{12,13},{14,15},{16,17},{18,... | collective-permute-start | bytes 27656 | tf_op jit(solution)/shard_map/ppermute | solution.py:19
  49.9 0.5 copy.51
  50.3 1.5 %collective-permute-start.5 = (f32[2,64,18,1]{1,0,3,2:T(2,128)S(1)}, f32[2,64,18,1]{1,0,3,2:T(2,128)S(1)}, u32[]{:S(2)}, u32[]{:S(2)}) collective-permute-start(f32[2,64,18,1]{1,0,3,2:T(2,128)S(1)} %copy.51), channel_id=1, source_target_pairs={{1,0},{3,2},{5,4},{7,6},{9,8},{11,10},{13,12},{15,14},{17,16},{19,... | collective-permute-start | bytes 27656 | tf_op jit(solution)/shard_map/ppermute | solution.py:22
  51.8 17.9 %all-reduce.2.cloned.1.call-done = f32[2,64,512]{2,1,0:T(8,128)} async-done(((f32[2,64,512]{2,1,0:T(8,128)}), f32[2,64,512]{2,1,0:T(8,128)}) %all-reduce.2.cloned.1.call-update) | async-done | bytes 262160 | tf_op jit(solution)/shard_map/psum | solution.py:50
  69.7 1.5 %fusion.22 = f32[2,64,1,512]{3,1,0,2:T(8,128)S(1)} fusion(f32[2,64,1,512]{3,1,0,2:T(8,128)} %copy-done.8, f32[2,64,512]{2,1,0:T(8,128)} %all-reduce.2.cloned.1.call-done, f32[2,64]{1,0:T(2,128)S(1)} %pad_maximum_fusion.13, pred[]{:T(512)S(6)} %eq.10, f32[32,64]{1,0:T(8,128)S(1)} %get-tuple-element.14, f32[32,64]{1,0:T(8,128)S(1)} %get-tuple-element.13, ...), kind=kOutput, calls=%fused_computation.46 | convolution fusion | flops 50597888 | bytes 1065473 | tf_op jit(solution)/shard_map/mt,cmr->ctr/dot_general | solution.py:51
  71.2 1.0 copy.46
  72.2 0.6 copy.50
  72.8 1.7 %copy.52 = f32[2,64,18,1]{3,2,1,0:T(8,128)} copy(f32[2,64,18,1]{1,0,3,2:T(2,128)S(1)} %collective-permute-done.5) | data formatting | bytes 18432 | tf_op jit(solution)/shard_map/ppermute | solution.py:22
  74.5 15.2 %fusion.1 = f32[2,64,16,512]{3,2,1,0:T(8,128)S(1)} fusion(f32[2,64,18,1]{3,2,1,0:T(8,128)} %copy.52, f32[2,64,1,512]{3,2,1,0:T(1,128)} %copy-done.6, f32[2,64,16,512]{3,2,1,0:T(8,128)} %param.8, f32[2,64,1,512]{3,2,1,0:T(1,128)S(1)} %copy-done.5, f32[2,64,18,1]{3,2,1,0:T(8,128)S(1)} %copy.50, f32[2,1,16,512]{3,2,1,0:T(8,128)} %collective-permute-done.1, ...), kind=kLoop, calls=%fused_computation.3 | loop fusion | flops 17825792 | bytes 13256704 | tf_op jit(solution)/shard_map/sub | solution.py:70
  89.7 2.5 %fusion.17 = (f32[1,64,16,512]{3,2,1,0:T(8,128)S(1)}, f32[64,16,512]{2,1,0:T(8,128)S(1)}) fusion(f32[2,64,16,512]{3,2,1,0:T(8,128)S(1)} %fusion.1, f32[2,64,16,512]{3,2,1,0:T(8,128)S(1)} %copy-done.2, f32[2,64,16,512]{3,2,1,0:T(8,128)S(1)} %copy-done.1, s32[64,16,512]{2,1,0:T(8,128)} %param.10, f32[64,16]{1,0:T(8,128)S(1)} %bitcast.71), kind=kLoop, calls=%fused_computation.31 | loop fusion | flops 7864320 | bytes 14684160 | tf_op jit(solution)/shard_map/stack | solution.py:96
  92.2 1.3 %fusion.12 = f32[1,64,16,512]{3,2,1,0:T(8,128)S(1)} fusion(f32[64,16,512]{2,1,0:T(8,128)S(1)} %bitcast.70, f32[64,16,512]{2,1,0:T(8,128)S(1)} %get-tuple-element.6, f32[2,64,16,512]{3,2,1,0:T(8,128)S(1)} %fusion.1, f32[2,64,16,512]{3,2,1,0:T(8,128)S(1)} %copy-done.2, f32[2,64,16,512]{3,2,1,0:T(8,128)S(1)} %copy-done.1), kind=kLoop, calls=%fused_computation.24 | loop fusion | flops 2621440 | bytes 12582912 | tf_op jit(solution)/shard_map/stack | solution.py:96
  93.6 2.5 %pad_maximum_fusion.9 = f32[2,64,16,512]{3,2,1,0:T(8,128)} fusion(f32[1,64,16,512]{3,2,1,0:T(8,128)S(1)} %fusion.12, f32[1,64,16,512]{3,2,1,0:T(8,128)S(1)} %get-tuple-element.5), kind=kLoop, calls=%fused_computation.18 | loop fusion | flops 1048576 | bytes 8388608 | tf_op jit(solution)/shard_map/stack | solution.py:96
  (44 shorter events, 0.3 us)
Async XLA Ops:
  6.5 16.2 %copy-start.10 = (f32[1,8,8]{2,1,0:T(8,128)S(1)}, f32[1,8,8]{2,1,0:T(8,128)}, u32[]{:S(2)}) copy-start(f32[1,8,8]{2,1,0:T(8,128)} %param.13) | copy-start | bytes 772
  6.5 16.2 %copy-start.9 = (f32[1,8,8,512]{3,2,1,0:T(8,128)S(1)}, f32[1,8,8,512]{3,2,1,0:T(8,128)}, u32[]{:S(2)}) copy-start(f32[1,8,8,512]{3,2,1,0:T(8,128)} %param.14) | copy-start | bytes 393220
  6.5 63.1 %all-reduce.2.cloned.1.call-start = ((), (), s32[]{:S(2)}) async-start(), calls=%async_computation.1 | async-start | bytes 524288 | tf_op jit(solution)/shard_map/psum | solution.py:50
  10.6 32.8 %collective-permute-start.3 = (f32[2,64,1,512]{3,1,0,2:T(8,128)S(1)}, f32[2,64,1,512]{3,1,0,2:T(8,128)S(1)}, u32[]{:S(2)}, u32[]{:S(2)}) collective-permute-start(f32[2,64,1,512]{3,1,0,2:T(8,128)S(1)} %copy.56), channel_id=1, source_target_pairs={{2,0},{3,1},{6,4},{7,5},{10,8},{11,9},{14,12},{15,13},{18,16},{19,... | collective-permute-start | bytes 786440 | tf_op jit(solution)/shard_map/ppermute | solution.py:22
  12.7 30.4 %collective-permute-start.2 = (f32[2,64,1,512]{3,1,0,2:T(8,128)}, f32[2,64,1,512]{3,1,0,2:T(8,128)S(1)}, u32[]{:S(2)}, u32[]{:S(2)}) collective-permute-start(f32[2,64,1,512]{3,1,0,2:T(8,128)} %copy.55), channel_id=1, source_target_pairs={{0,2},{1,3},{4,6},{5,7},{8,10},{9,11},{12,14},{13,15},{16,18},{17,... | collective-permute-start | bytes 786440 | tf_op jit(solution)/shard_map/ppermute | solution.py:19
  19.1 14.0 %collective-permute-start = (f32[2,1,16,512]{3,2,1,0:T(8,128)S(1)}, f32[2,1,16,512]{3,2,1,0:T(8,128)S(1)}, u32[]{:S(2)}, u32[]{:S(2)}) collective-permute-start(f32[2,1,16,512]{3,2,1,0:T(8,128)S(1)} %get-tuple-element.9), channel_id=1, source_target_pairs={{0,4},{4,8},{8,12},{12,16},{16,20},{20,24},{24,28},{28,0},{1,5},{5... | collective-permute-start | bytes 196616 | tf_op jit(solution)/shard_map/ppermute | solution.py:19
  19.1 55.3 %collective-permute-start.1 = (f32[2,1,16,512]{3,2,1,0:T(8,128)}, f32[2,1,16,512]{3,2,1,0:T(8,128)}, u32[]{:S(2)}, u32[]{:S(2)}) collective-permute-start(f32[2,1,16,512]{3,2,1,0:T(8,128)} %get-tuple-element.10), channel_id=1, source_target_pairs={{4,0},{8,4},{12,8},{16,12},{20,16},{24,20},{28,24},{0,28},{5,1},{9... | collective-permute-start | bytes 196616 | tf_op jit(solution)/shard_map/ppermute | solution.py:22
  23.5 16.6 %all-to-all-start = ((f32[8,8,512]{2,1,0:T(8,128)}), f32[8,8,512]{2,1,0:T(8,128)S(1)}, u32[]{:S(2)}, u32[]{:S(2)}) async-start(f32[8,8,512]{2,1,0:T(8,128)} %bitcast_multiply_fusion.2), calls=%async_computation | async-start | bytes 262144 | tf_op jit(solution)/shard_map/all_to_all | solution.py:81
  27.6 5.3 %copy-start.12 = (s32[4,16]{1,0:T(4,128)S(1)}, s32[4,16]{1,0:T(4,128)}, u32[]{:S(2)}) copy-start(s32[4,16]{1,0:T(4,128)} %param.11) | copy-start | bytes 772
  27.6 5.3 %copy-start.11 = (s32[1,8,8]{2,1,0:T(8,128)S(1)}, s32[1,8,8]{2,1,0:T(8,128)}, u32[]{:S(2)}) copy-start(s32[1,8,8]{2,1,0:T(8,128)} %param.15) | copy-start | bytes 772
  27.6 5.4 %copy-start.13 = (f32[2,32]{1,0:T(2,128)S(1)}, f32[2,32]{1,0:T(2,128)}, u32[]{:S(2)}) copy-start(f32[2,32]{1,0:T(2,128)} %param.12) | copy-start | bytes 772
  27.6 5.5 %copy-start.7 = (f32[64,16,512]{2,1,0:T(8,128)S(1)}, f32[64,16,512]{2,1,0:T(8,128)}, u32[]{:S(2)}) copy-start(f32[64,16,512]{2,1,0:T(8,128)} %param.9) | copy-start | bytes 6291460
  41.5 3.1 %copy-start = (f32[2,64,16,512]{3,2,1,0:T(8,128)S(1)}, f32[2,64,16,512]{3,2,1,0:T(8,128)}, u32[]{:S(2)}) copy-start(f32[2,64,16,512]{3,2,1,0:T(8,128)} %param.8) | copy-start | bytes 12582916
  43.4 2.3 %copy-start.4 = (f32[2,64,1,512]{3,2,1,0:T(1,128)}, f32[2,64,1,512]{3,2,1,0:T(1,128)S(1)}, u32[]{:S(2)}) copy-start(f32[2,64,1,512]{3,2,1,0:T(1,128)S(1)} %copy.43) | copy-start | bytes 786436
  43.4 0.7 copy-start.8
  44.7 1.0 copy-start.6
  46.1 26.0 %collective-permute-start.4 = (f32[2,64,18,1]{1,0,3,2:T(2,128)S(1)}, f32[2,64,18,1]{1,0,3,2:T(2,128)S(1)}, u32[]{:S(2)}, u32[]{:S(2)}) collective-permute-start(f32[2,64,18,1]{1,0,3,2:T(2,128)S(1)} %copy.49), channel_id=1, source_target_pairs={{0,1},{2,3},{4,5},{6,7},{8,9},{10,11},{12,13},{14,15},{16,17},{18,... | collective-permute-start | bytes 27656 | tf_op jit(solution)/shard_map/ppermute | solution.py:19
  50.3 22.4 %collective-permute-start.5 = (f32[2,64,18,1]{1,0,3,2:T(2,128)S(1)}, f32[2,64,18,1]{1,0,3,2:T(2,128)S(1)}, u32[]{:S(2)}, u32[]{:S(2)}) collective-permute-start(f32[2,64,18,1]{1,0,3,2:T(2,128)S(1)} %copy.51), channel_id=1, source_target_pairs={{1,0},{3,2},{5,4},{7,6},{9,8},{11,10},{13,12},{15,14},{17,16},{19,... | collective-permute-start | bytes 27656 | tf_op jit(solution)/shard_map/ppermute | solution.py:22
  71.2 3.3 %copy-start.5 = (f32[2,64,1,512]{3,2,1,0:T(1,128)S(1)}, f32[2,64,1,512]{3,2,1,0:T(1,128)}, u32[]{:S(2)}) copy-start(f32[2,64,1,512]{3,2,1,0:T(1,128)} %copy-done.4) | copy-start | bytes 786436
  74.4 15.2 %copy-start.2 = (f32[2,64,16,512]{3,2,1,0:T(8,128)S(1)}, f32[2,64,16,512]{3,2,1,0:T(8,128)}, u32[]{:S(2)}) copy-start(f32[2,64,16,512]{3,2,1,0:T(8,128)} %fusion.7) | copy-start | bytes 12582916
  74.4 15.2 %copy-start.1 = (f32[2,64,16,512]{3,2,1,0:T(8,128)S(1)}, f32[2,64,16,512]{3,2,1,0:T(8,128)}, u32[]{:S(2)}) copy-start(f32[2,64,16,512]{3,2,1,0:T(8,128)} %param.8) | copy-start | bytes 12582916
  89.7 2.5 %copy-start.3 = (f32[1024,512]{1,0:T(8,128)S(1)}, f32[1024,512]{1,0:T(8,128)}, u32[]{:S(2)}) copy-start(f32[1024,512]{1,0:T(8,128)} %broadcast_multiply_fusion) | copy-start | bytes 6291460
Sparse Core Ops, SparseCore 0:
  10.7 58.8 all-reduce.1
where the time goes:
time: 103 us
  other arithmetic  33.4 us (32%)
  starting transfers between devices  19.1 us (19%)
  waiting for transfers between devices  17.9 us (17%)
  local copies, waits for them, and re-layouts  16.1 us (16%)
  between operations  13.7 us (13%)
  matrix products  2.57 us (2%)
    psum x1, waiting for transfers between devices, body(): mode_sums = lax.psum(partial_value, 'azi')  17.9 us
    sub x1, other arithmetic, body(): theta_prev + theta_next + axial_prev + axial_next + radial_prev  15.2 us
    ppermute x3, starting transfers between devices, with_halo(): lax.ppermute(lax.slice_in_dim(block, block.shape[dim] - width, None, axis...  8.62 us
    mul x1, other arithmetic, body(): upwind_term = swirl_speed[None] * (fields - theta_prev)  6.95 us
    ppermute x3, starting transfers between devices, with_halo(): lax.ppermute(lax.slice_in_dim(block, 0, width, axis=dim), axis, backward)  6.36 us
    another operation x3, other arithmetic, body(): return jnp.stack([new_energy, new_fuel], axis=0)  6.28 us
    slice x1, local copies, waits for them, and re-layouts, body(): axial_inner[:, :, :-1, :]  5.25 us
    slice x3, local copies, waits for them, and re-layouts, with_halo(): lax.slice_in_dim(block, block.shape[dim] - width, None, axis=dim)  4.75 us
  transfers between devices with their start and end apart: 8, of which 1 were waited for; matrix products, arithmetic and copies ran while one was open for 25% of the time, Pallas kernels for 0%

commit v1 on v0

--- a/solution.py
+++ b/solution.py
@@ -47,7 +47,8 @@
         "mt,ctr->cmr", phase_rows, outlet_plane, precision=lax.Precision.HIGHEST
     )
     gain_both = jnp.concatenate([outlet_gain, outlet_gain], axis=1)
-    mode_sums = lax.psum(partial_value, "azi")
+    manage_series_all = lambda obj: jnp.sum(lax.all_gather(obj, "azi"), axis=0)
+    mode_sums = manage_series_all(partial_value)
     rebuilt = jnp.einsum(
         "mt,cmr->ctr",
         phase_rows,

time: 103 us -> 96.2 us (0.934)
  waiting for transfers between devices: 17.9 us -> 1.6 us
  other arithmetic: 33.4 us -> 39 us
  local copies, waits for them, and re-layouts: 16.1 us -> 19.5 us
  starting transfers between devices: 19.1 us -> 20.4 us
    psum x1 -> x0, waiting for transfers between devices: 17.9 us -> none  [body(): mode_sums = lax.psum(partial_value, 'azi')]
    slice x1, other arithmetic: 0.99 us -> 4.13 us  [with_halo(): lax.slice_in_dim(block, block.shape[dim] - width, None, axis=dim)]
    slice x1, local copies, waits for them, and re-layouts: 0.46 us -> 2.41 us  [with_halo(): lax.slice_in_dim(block, 0, width, axis=dim)]
    reduce_sum x0 -> x1, other arithmetic: none -> 1.82 us  [body(): manage_series_all = lambda obj: jnp.sum(lax.all_gather(obj, 'azi'), axis=0)]
    unnamed x30 -> x28, local copies, waits for them, and re-layouts: 1.81 us -> 0.1 us
    ppermute x2, local copies, waits for them, and re-layouts: 0.85 us -> 2.52 us  [with_halo(): lax.ppermute(lax.slice_in_dim(block, block.shape[dim] - width, None, axis...]
    ppermute x3, waiting for transfers between devices: 0.01 us -> 1.58 us  [with_halo(): lax.ppermute(lax.slice_in_dim(block, 0, width, axis=dim), axis, backward)]
    slice x3, local copies, waits for them, and re-layouts: 4.75 us -> 6.1 us  [with_halo(): lax.slice_in_dim(block, block.shape[dim] - width, None, axis=dim)]
  transfers between devices with their start and end apart: 8 -> 8, of which waited for: 1 -> 1; matrix products, arithmetic and copies ran while one was open for 25% -> 35% of each run, Pallas kernels for 0% -> 0%
where the time goes in v1:
time: 96.2 us; the launch traced here: 95.6 us
  other arithmetic  39 us (41%)
  starting transfers between devices  20.4 us (21%)
  local copies, waits for them, and re-layouts  19.5 us (20%)
  between operations  13.7 us (14%)
  waiting for transfers between devices  1.6 us (2%)
  matrix products  1.55 us (2%)
    sub x1, other arithmetic, body(): theta_prev + theta_next + axial_prev + axial_next + radial_prev  15.7 us
    ppermute x3, starting transfers between devices, with_halo(): lax.ppermute(lax.slice_in_dim(block, block.shape[dim] - width, None, axis...  9.85 us
    mul x1, other arithmetic, body(): upwind_term = swirl_speed[None] * (fields - theta_prev)  6.98 us
    ppermute x3, starting transfers between devices, with_halo(): lax.ppermute(lax.slice_in_dim(block, 0, width, axis=dim), axis, backward)  6.35 us
    another operation x3, other arithmetic, body(): return jnp.stack([new_energy, new_fuel], axis=0)  6.28 us
    slice x3, local copies, waits for them, and re-layouts, with_halo(): lax.slice_in_dim(block, block.shape[dim] - width, None, axis=dim)  6.1 us
    slice x1, local copies, waits for them, and re-layouts, body(): axial_inner[:, :, :-1, :]  5.27 us
    all_to_all x1, starting transfers between devices, body(): lax.all_to_all(payload, 'azi', split_axis=0, concat_axis=0, tiled=True)  4.14 us
  transfers between devices with their start and end apart: 8, of which 1 were waited for; matrix products, arithmetic and copies ran while one was open for 35% of the time, Pallas kernels for 0%

profile of v1, /device:TPU:0, one launch (start us, length us, event | category | flops | bytes accessed | tf_op | source)
XLA Modules:
  0.0 95.6 jit_solution(17439996115639894036)
XLA Ops:
  6.5 2.8 %fusion.38 = (f32[2,64,1,512]{3,2,1,0:T(1,128)S(1)}, f32[2,64,1,512]{3,2,1,0:T(1,128)S(1)}) fusion(f32[2,64,16,512]{3,2,1,0:T(8,128)} %param.8), kind=kLoop, calls=%fused_computation.80 | loop fusion | bytes 1048576 | tf_op jit(solution)/shard_map/slice | solution.py:20
  9.3 0.2 fusion.31
  9.5 1.1 %convolution_bitcast_fusion = f32[2,64,512]{2,1,0:T(8,128)} fusion(f32[32,64]{1,0:T(8,128)S(1)} %get-tuple-element.14, f32[32,64]{1,0:T(8,128)S(1)} %get-tuple-element.13, f32[2,64,1,512]{3,2,1,0:T(1,128)S(1)} %get-tuple-element.11), kind=kOutput, calls=%fused_computation.41 | convolution fusion | flops 50335744 | bytes 540672 | tf_op jit(solution)/shard_map/mt,ctr->cmr/dot_general | solution.py:46
  10.6 1.3 %collective-permute-start.3 = (f32[2,64,1,512]{3,1,0,2:T(8,128)S(1)}, f32[2,64,1,512]{3,1,0,2:T(8,128)S(1)}, u32[]{:S(2)}, u32[]{:S(2)}) collective-permute-start(f32[2,64,1,512]{3,1,0,2:T(8,128)S(1)} %copy.58), channel_id=1, source_target_pairs={{2,0},{3,1},{6,4},{7,5},{10,8},{11,9},{14,12},{15,13},{18,16},{19,... | collective-permute-start | bytes 786440 | tf_op jit(solution)/shard_map/ppermute | solution.py:22
  12.0 5.6 %collective-permute-start.2 = (f32[2,64,1,512]{3,1,0,2:T(8,128)S(1)}, f32[2,64,1,512]{3,1,0,2:T(8,128)}, u32[]{:S(2)}, u32[]{:S(2)}) collective-permute-start(f32[2,64,1,512]{3,1,0,2:T(8,128)S(1)} %copy.57), channel_id=1, source_target_pairs={{0,2},{1,3},{4,6},{5,7},{8,10},{9,11},{12,14},{13,15},{16,18},{17,... | collective-permute-start | bytes 786440 | tf_op jit(solution)/shard_map/ppermute | solution.py:19
  17.6 1.5 %fusion.37 = (f32[2,1,16,512]{3,2,1,0:T(8,128)}, f32[2,1,16,512]{3,2,1,0:T(8,128)S(1)}) fusion(f32[2,64,16,512]{3,2,1,0:T(8,128)} %param.8), kind=kLoop, calls=%fused_computation.79 | loop fusion | bytes 262144 | tf_op jit(solution)/shard_map/slice | solution.py:20
  19.1 3.6 %collective-permute-start.1 = (f32[2,1,16,512]{3,2,1,0:T(8,128)S(1)}, f32[2,1,16,512]{3,2,1,0:T(8,128)S(1)}, u32[]{:S(2)}, u32[]{:S(2)}) collective-permute-start(f32[2,1,16,512]{3,2,1,0:T(8,128)S(1)} %get-tuple-element.10), channel_id=1, source_target_pairs={{4,0},{8,4},{12,8},{16,12},{20,16},{24,20},{28,24},{0,28},{5,1},{9... | collective-permute-start | bytes 196616 | tf_op jit(solution)/shard_map/ppermute | solution.py:22
  22.7 0.7 bitcast_multiply_fusion.2
  23.4 4.1 %all-to-all-start = ((f32[8,8,512]{2,1,0:T(8,128)}), f32[8,8,512]{2,1,0:T(8,128)S(1)}, u32[]{:S(2)}, u32[]{:S(2)}) async-start(f32[8,8,512]{2,1,0:T(8,128)} %bitcast_multiply_fusion.2), calls=%async_computation | async-start | bytes 262144 | tf_op jit(solution)/shard_map/all_to_all | solution.py:82
  27.6 5.3 %slice.74 = f32[2,64,15,512]{3,2,1,0:T(8,128)} slice(f32[2,64,16,512]{3,2,1,0:T(8,128)} %param.8), slice={[0:2], [0:64], [1:16], [0:512]} | slice | bytes 7864320 | tf_op jit(solution)/shard_map/slice | solution.py:69
  32.9 0.1 squeeze.26
  33.0 0.1 pad_maximum_fusion.13
  33.1 7.0 %fusion.7 = f32[2,64,16,512]{3,2,1,0:T(8,128)} fusion(f32[2,64,16,512]{3,2,1,0:T(8,128)} %param.8, f32[2,1,16,512]{3,2,1,0:T(8,128)S(1)} %collective-permute-done, f32[64,16,512]{2,1,0:T(8,128)S(1)} %copy-done.5), kind=kLoop, calls=%fused_computation.17 | loop fusion | flops 3145728 | bytes 10551296 | tf_op jit(solution)/shard_map/mul | solution.py:73
  40.1 1.5 %scatter_custom_fusion = f32[1024,512]{1,0:T(8,128)S(1)} fusion(s32[64]{0:T(128)S(1)} %fusion.33, f32[]{:T(128)} %constant.71.clone.1, f32[8,8,512]{2,1,0:T(8,128)S(1)} %all-to-all-done), kind=kCustom, calls=%fused_computation.43 | custom fusion | flops 32768 | bytes 2228228 | tf_op jit(solution)/shard_map/scatter-add | solution.py:89
  41.6 1.2 %copy.45 = f32[2,64,1,512]{3,2,1,0:T(1,128)S(1)} copy(f32[2,64,1,512]{3,1,0,2:T(8,128)} %collective-permute-done.2) | data formatting | bytes 524288 | tf_op jit(solution)/shard_map/ppermute | solution.py:19
  42.8 0.3 copy.50
  43.1 4.1 %pad_maximum_fusion.12 = (f32[2,64,18,1]{3,2,1,0:T(8,128)}, f32[2,64,18,1]{3,2,1,0:T(8,128)}) fusion(f32[2,64,1,512]{3,2,1,0:T(1,128)S(1)} %copy.50, f32[2,64,16,512]{3,2,1,0:T(8,128)} %param.8, f32[2,64,1,512]{3,2,1,0:T(1,128)S(1)} %copy.45), kind=kLoop, calls=%fused_computation.37 | loop fusion | flops 9216 | bytes 4737024 | tf_op jit(solution)/shard_map/slice | solution.py:20
  47.2 1.8 %copy.51 = f32[2,64,18,1]{1,0,3,2:T(2,128)S(1)} copy(f32[2,64,18,1]{3,2,1,0:T(8,128)} %get-tuple-element.7) | data formatting | bytes 18432 | tf_op jit(solution)/shard_map/slice | solution.py:20
  49.1 4.2 %collective-permute-start.4 = (f32[2,64,18,1]{1,0,3,2:T(2,128)S(1)}, f32[2,64,18,1]{1,0,3,2:T(2,128)}, u32[]{:S(2)}, u32[]{:S(2)}) collective-permute-start(f32[2,64,18,1]{1,0,3,2:T(2,128)S(1)} %copy.51), channel_id=1, source_target_pairs={{0,1},{2,3},{4,5},{6,7},{8,9},{10,11},{12,13},{14,15},{16,17},{18,... | collective-permute-start | bytes 27656 | tf_op jit(solution)/shard_map/ppermute | solution.py:19
  53.3 2.4 %copy.53 = f32[2,64,18,1]{1,0,3,2:T(2,128)} copy(f32[2,64,18,1]{3,2,1,0:T(8,128)} %get-tuple-element.8) | data formatting | bytes 18432 | tf_op jit(solution)/shard_map/slice | solution.py:22
  55.7 1.5 %collective-permute-start.5 = (f32[2,64,18,1]{1,0,3,2:T(2,128)}, f32[2,64,18,1]{1,0,3,2:T(2,128)}, u32[]{:S(2)}, u32[]{:S(2)}) collective-permute-start(f32[2,64,18,1]{1,0,3,2:T(2,128)} %copy.53), channel_id=1, source_target_pairs={{1,0},{3,2},{5,4},{7,6},{9,8},{11,10},{13,12},{15,14},{17,16},{19,... | collective-permute-start | bytes 27656 | tf_op jit(solution)/shard_map/ppermute | solution.py:22
  57.2 1.6 %broadcast_multiply_fusion = f32[1024,512]{1,0:T(8,128)} fusion(f32[1024,512]{1,0:T(8,128)S(1)} %scatter_custom_fusion, f32[]{:T(128)S(6)} %convert_element_type.21), kind=kLoop, calls=%fused_computation.42 | loop fusion | flops 524288 | bytes 4194308 | tf_op jit(solution)/shard_map/mul | solution.py:92
  58.8 1.3 %copy.52 = f32[2,64,18,1]{3,2,1,0:T(8,128)S(1)} copy(f32[2,64,18,1]{1,0,3,2:T(2,128)} %collective-permute-done.4) | data formatting | bytes 18432 | tf_op jit(solution)/shard_map/ppermute | solution.py:19
  60.1 1.6 %collective-permute-done.5 = f32[2,64,18,1]{1,0,3,2:T(2,128)} collective-permute-done((f32[2,64,18,1]{1,0,3,2:T(2,128)}, f32[2,64,18,1]{1,0,3,2:T(2,128)}, u32[]{:S(2)}, u32[]{:S(2)}) %collective-permute-start.5) | collective-permute-done | bytes 9248 | tf_op jit(solution)/shard_map/ppermute | solution.py:22
  61.7 2.5 %copy.54 = f32[2,64,18,1]{3,2,1,0:T(8,128)} copy(f32[2,64,18,1]{1,0,3,2:T(2,128)} %collective-permute-done.5) | data formatting | bytes 18432 | tf_op jit(solution)/shard_map/ppermute | solution.py:22
  64.1 1.8 %reduce_sum.9 = f32[2,64,512]{2,1,0:T(8,128)S(1)} reduce(f32[8,2,64,512]{3,2,1,0:T(8,128)} %bitcast.72, f32[]{:T(128)} %constant.71.clone.1), dimensions={0}, to_apply=%region_0.1 | reduce | flops 458752 | bytes 2359300 | tf_op jit(solution)/shard_map/reduce_sum | solution.py:50
  66.0 0.5 fusion.22
  66.4 0.3 copy.48
  66.7 15.7 %fusion.1 = f32[2,64,16,512]{3,2,1,0:T(8,128)S(1)} fusion(f32[2,64,18,1]{3,2,1,0:T(8,128)} %copy.54, f32[2,64,1,512]{3,2,1,0:T(1,128)} %copy-done.4, f32[2,64,16,512]{3,2,1,0:T(8,128)} %param.8, f32[2,64,1,512]{3,2,1,0:T(1,128)} %copy-done.3, f32[2,64,18,1]{3,2,1,0:T(8,128)S(1)} %copy.52, f32[2,1,16,512]{3,2,1,0:T(8,128)S(1)} %collective-permute-done.1, ...), kind=kLoop, calls=%fused_computation.3 | loop fusion | flops 17825792 | bytes 13256704 | tf_op jit(solution)/shard_map/sub | solution.py:71
  82.5 2.5 %fusion.17 = (f32[1,64,16,512]{3,2,1,0:T(8,128)S(1)}, f32[64,16,512]{2,1,0:T(8,128)S(1)}) fusion(f32[2,64,16,512]{3,2,1,0:T(8,128)S(1)} %fusion.1, f32[2,64,16,512]{3,2,1,0:T(8,128)S(1)} %copy-done.1, f32[2,64,16,512]{3,2,1,0:T(8,128)S(1)} %copy-done, s32[64,16,512]{2,1,0:T(8,128)} %param.10, f32[64,16]{1,0:T(8,128)S(1)} %bitcast.73), kind=kLoop, calls=%fused_computation.31 | loop fusion | flops 7864320 | bytes 14684160 | tf_op jit(solution)/shard_map/stack | solution.py:97
  85.0 1.3 %fusion.12 = f32[1,64,16,512]{3,2,1,0:T(8,128)S(1)} fusion(f32[64,16,512]{2,1,0:T(8,128)S(1)} %bitcast.71, f32[64,16,512]{2,1,0:T(8,128)S(1)} %get-tuple-element.6, f32[2,64,16,512]{3,2,1,0:T(8,128)S(1)} %fusion.1, f32[2,64,16,512]{3,2,1,0:T(8,128)S(1)} %copy-done.1, f32[2,64,16,512]{3,2,1,0:T(8,128)S(1)} %copy-done), kind=kLoop, calls=%fused_computation.24 | loop fusion | flops 2621440 | bytes 12582912 | tf_op jit(solution)/shard_map/stack | solution.py:97
  86.3 2.5 %pad_maximum_fusion.9 = f32[2,64,16,512]{3,2,1,0:T(8,128)} fusion(f32[1,64,16,512]{3,2,1,0:T(8,128)S(1)} %fusion.12, f32[1,64,16,512]{3,2,1,0:T(8,128)S(1)} %get-tuple-element.5), kind=kLoop, calls=%fused_computation.18 | loop fusion | flops 1048576 | bytes 8388608 | tf_op jit(solution)/shard_map/stack | solution.py:97
  (43 shorter events, 0.2 us)
Async XLA Ops:
  6.5 16.1 %copy-start.9 = (f32[1,8,8]{2,1,0:T(8,128)S(1)}, f32[1,8,8]{2,1,0:T(8,128)}, u32[]{:S(2)}) copy-start(f32[1,8,8]{2,1,0:T(8,128)} %param.13) | copy-start | bytes 772
  6.5 16.1 %copy-start.8 = (f32[1,8,8,512]{3,2,1,0:T(8,128)S(1)}, f32[1,8,8,512]{3,2,1,0:T(8,128)}, u32[]{:S(2)}) copy-start(f32[1,8,8,512]{3,2,1,0:T(8,128)} %param.14) | copy-start | bytes 393220
  6.5 57.6 %all-gather.3.cloned.1.call-start = ((), (), s32[]{:S(2)}) async-start(), calls=%async_computation.1 | async-start | bytes 2359296 | tf_op jit(solution)/shard_map/all_gather | solution.py:50
  10.6 32.2 %collective-permute-start.3 = (f32[2,64,1,512]{3,1,0,2:T(8,128)S(1)}, f32[2,64,1,512]{3,1,0,2:T(8,128)S(1)}, u32[]{:S(2)}, u32[]{:S(2)}) collective-permute-start(f32[2,64,1,512]{3,1,0,2:T(8,128)S(1)} %copy.58), channel_id=1, source_target_pairs={{2,0},{3,1},{6,4},{7,5},{10,8},{11,9},{14,12},{15,13},{18,16},{19,... | collective-permute-start | bytes 786440 | tf_op jit(solution)/shard_map/ppermute | solution.py:22
  12.0 29.6 %collective-permute-start.2 = (f32[2,64,1,512]{3,1,0,2:T(8,128)S(1)}, f32[2,64,1,512]{3,1,0,2:T(8,128)}, u32[]{:S(2)}, u32[]{:S(2)}) collective-permute-start(f32[2,64,1,512]{3,1,0,2:T(8,128)S(1)} %copy.57), channel_id=1, source_target_pairs={{0,2},{1,3},{4,6},{5,7},{8,10},{9,11},{12,14},{13,15},{16,18},{17,... | collective-permute-start | bytes 786440 | tf_op jit(solution)/shard_map/ppermute | solution.py:19
  19.1 14.0 %collective-permute-start = (f32[2,1,16,512]{3,2,1,0:T(8,128)}, f32[2,1,16,512]{3,2,1,0:T(8,128)S(1)}, u32[]{:S(2)}, u32[]{:S(2)}) collective-permute-start(f32[2,1,16,512]{3,2,1,0:T(8,128)} %get-tuple-element.9), channel_id=1, source_target_pairs={{0,4},{4,8},{8,12},{12,16},{16,20},{20,24},{24,28},{28,0},{1,5},{5... | collective-permute-start | bytes 196616 | tf_op jit(solution)/shard_map/ppermute | solution.py:19
  19.1 47.7 %collective-permute-start.1 = (f32[2,1,16,512]{3,2,1,0:T(8,128)S(1)}, f32[2,1,16,512]{3,2,1,0:T(8,128)S(1)}, u32[]{:S(2)}, u32[]{:S(2)}) collective-permute-start(f32[2,1,16,512]{3,2,1,0:T(8,128)S(1)} %get-tuple-element.10), channel_id=1, source_target_pairs={{4,0},{8,4},{12,8},{16,12},{20,16},{24,20},{28,24},{0,28},{5,1},{9... | collective-permute-start | bytes 196616 | tf_op jit(solution)/shard_map/ppermute | solution.py:22
  23.4 16.7 %all-to-all-start = ((f32[8,8,512]{2,1,0:T(8,128)}), f32[8,8,512]{2,1,0:T(8,128)S(1)}, u32[]{:S(2)}, u32[]{:S(2)}) async-start(f32[8,8,512]{2,1,0:T(8,128)} %bitcast_multiply_fusion.2), calls=%async_computation | async-start | bytes 262144 | tf_op jit(solution)/shard_map/all_to_all | solution.py:82
  27.6 5.3 %copy-start.10 = (s32[1,8,8]{2,1,0:T(8,128)S(1)}, s32[1,8,8]{2,1,0:T(8,128)}, u32[]{:S(2)}) copy-start(s32[1,8,8]{2,1,0:T(8,128)} %param.15) | copy-start | bytes 772
  27.6 5.4 %copy-start.11 = (s32[4,16]{1,0:T(4,128)S(1)}, s32[4,16]{1,0:T(4,128)}, u32[]{:S(2)}) copy-start(s32[4,16]{1,0:T(4,128)} %param.11) | copy-start | bytes 772
  27.6 5.4 %copy-start.12 = (f32[2,32]{1,0:T(2,128)S(1)}, f32[2,32]{1,0:T(2,128)}, u32[]{:S(2)}) copy-start(f32[2,32]{1,0:T(2,128)} %param.12) | copy-start | bytes 772
  27.6 5.5 %copy-start.5 = (f32[64,16,512]{2,1,0:T(8,128)S(1)}, f32[64,16,512]{2,1,0:T(8,128)}, u32[]{:S(2)}) copy-start(f32[64,16,512]{2,1,0:T(8,128)} %param.9) | copy-start | bytes 6291460
  42.8 4.5 %copy-start.3 = (f32[2,64,1,512]{3,2,1,0:T(1,128)}, f32[2,64,1,512]{3,2,1,0:T(1,128)S(1)}, u32[]{:S(2)}) copy-start(f32[2,64,1,512]{3,2,1,0:T(1,128)S(1)} %copy.45) | copy-start | bytes 786436
  42.8 4.4 %copy-start.6 = (f32[2,64,1,512]{3,1,0,2:T(8,128)}, f32[2,64,1,512]{3,1,0,2:T(8,128)S(1)}, u32[]{:S(2)}) copy-start(f32[2,64,1,512]{3,1,0,2:T(8,128)S(1)} %collective-permute-done.3) | copy-start | bytes 786436
  43.1 4.1 %copy-start.4 = (f32[2,64,1,512]{3,2,1,0:T(1,128)}, f32[2,64,1,512]{3,2,1,0:T(1,128)S(1)}, u32[]{:S(2)}) copy-start(f32[2,64,1,512]{3,2,1,0:T(1,128)S(1)} %copy.50) | copy-start | bytes 786436
  49.1 9.7 %collective-permute-start.4 = (f32[2,64,18,1]{1,0,3,2:T(2,128)S(1)}, f32[2,64,18,1]{1,0,3,2:T(2,128)}, u32[]{:S(2)}, u32[]{:S(2)}) collective-permute-start(f32[2,64,18,1]{1,0,3,2:T(2,128)S(1)} %copy.51), channel_id=1, source_target_pairs={{0,1},{2,3},{4,5},{6,7},{8,9},{10,11},{12,13},{14,15},{16,17},{18,... | collective-permute-start | bytes 27656 | tf_op jit(solution)/shard_map/ppermute | solution.py:19
  55.7 6.0 %collective-permute-start.5 = (f32[2,64,18,1]{1,0,3,2:T(2,128)}, f32[2,64,18,1]{1,0,3,2:T(2,128)}, u32[]{:S(2)}, u32[]{:S(2)}) collective-permute-start(f32[2,64,18,1]{1,0,3,2:T(2,128)} %copy.53), channel_id=1, source_target_pairs={{1,0},{3,2},{5,4},{7,6},{9,8},{11,10},{13,12},{15,14},{17,16},{19,... | collective-permute-start | bytes 27656 | tf_op jit(solution)/shard_map/ppermute | solution.py:22
  60.1 5.9 %copy-start.7 = (f32[2,64,1,512]{3,1,0,2:T(8,128)S(1)}, f32[2,64,1,512]{3,1,0,2:T(8,128)}, u32[]{:S(2)}) copy-start(f32[2,64,1,512]{3,1,0,2:T(8,128)} %copy-done.6) | copy-start | bytes 786436
  66.7 15.8 %copy-start.1 = (f32[2,64,16,512]{3,2,1,0:T(8,128)S(1)}, f32[2,64,16,512]{3,2,1,0:T(8,128)}, u32[]{:S(2)}) copy-start(f32[2,64,16,512]{3,2,1,0:T(8,128)} %fusion.7) | copy-start | bytes 12582916
  66.7 15.7 %copy-start = (f32[2,64,16,512]{3,2,1,0:T(8,128)S(1)}, f32[2,64,16,512]{3,2,1,0:T(8,128)}, u32[]{:S(2)}) copy-start(f32[2,64,16,512]{3,2,1,0:T(8,128)} %param.8) | copy-start | bytes 12582916
  82.5 2.5 %copy-start.2 = (f32[1024,512]{1,0:T(8,128)S(1)}, f32[1024,512]{1,0:T(8,128)}, u32[]{:S(2)}) copy-start(f32[1024,512]{1,0:T(8,128)} %broadcast_multiply_fusion) | copy-start | bytes 6291460
Sparse Core Ops, SparseCore 0:
  10.7 35.9 all-gather.2
